TPU v7x, 32 devices: a whole 2x2x4 slice. The times are simulated.
32 devices in a mesh: expert: 8 (over z, core), row: 4 (over y, x).
Axes of the slice: x: 2, y: 2, z: 4, core: 2. Of those that a mesh axis runs over, the one named last changes fastest.
Arguments:
- grads: bfloat16 [8, 7168, 2048], P('expert', 'row')
- basis: bfloat16 [8, 7168, 256], P('expert', 'row'), may hold values from -0.0625 to 0.0625
- loads: int32 [8], P('expert'), may hold values from 1 to 1, as said below
- flags: int32 [8], P('expert'), may hold values 0 or 1
Outputs:
- new_basis: float32 [8, 7168, 256], P('expert', 'row')
- rotated: float32 [8, 256, 2048], P('expert', None, 'row')
Inputs may be any that keep to these rules, and one draw needn't show every extreme that they name: Slots 0 to loads[d] - 1 of expert-axis index d are live and hold experts; the others are empty. Some index has all 1 slots live.
All inputs are finite; a program needn't handle non-finite values. No bound on the sum of `flags` on one device may be relied on, other than what follows from the above.
Results may differ from a plain program's by a relative error of at most 0.006.
Values sent between devices are 32-bit elements; how exact they have to be, the bound alone decides.
A program may use at most 64 MiB of HBM per device.

v0:
```python
import jax
import jax.numpy as jnp
from jax import lax
from jax.sharding import PartitionSpec as P

D = 7168
S = 2048


def on_device(grads, basis, loads, flags):
    slot_count = grads.shape[0]
    live_count = loads[0]
    live_mask = jnp.arange(slot_count, dtype=jnp.int32) < live_count
    refresh = jnp.logical_and(live_mask, flags == 1)
    live_cube = live_mask[:, None, None]
    refresh_cube = refresh[:, None, None]
    squares = jnp.sum(jnp.where(live_cube, jnp.square(grads.astype(jnp.float32)), 0.0))
    leader = (lax.axis_index("row") == 0).astype(jnp.float32)
    total_sq, total_live = lax.psum(
        (squares, leader * live_count.astype(jnp.float32)), ("expert", "row")
    )
    norm_scale = lax.rsqrt(total_sq / (total_live * D * S) + 1e-06)
    local_inner = jnp.einsum("cds,cdk->csk", grads, basis, preferred_element_type=jnp.float32)
    inner_sum = jnp.stack([lax.psum(local_inner[0], "row")])
    inner_gram = jnp.einsum("csk,csj->ckj", inner_sum, inner_sum, precision=lax.Precision.HIGHEST)
    inner_half = inner_sum.astype(jnp.bfloat16)
    power_rows = jnp.einsum(
        "cds,csk->cdk", grads, inner_half, preferred_element_type=jnp.float32
    ).astype(jnp.bfloat16)
    projector = jnp.where(refresh_cube, power_rows, basis)
    local_cross = jnp.einsum("cdk,cds->cks", projector, grads, preferred_element_type=jnp.float32)
    identity = jnp.eye(basis.shape[2], dtype=jnp.float32)
    lower_first = jnp.linalg.cholesky(jnp.where(refresh_cube, inner_gram, identity))
    first_rows = lax.linalg.triangular_solve(
        lower_first, power_rows.astype(jnp.float32), left_side=False, lower=True, transpose_a=True
    )
    local_second = jnp.einsum(
        "cdk,cdj->ckj", first_rows, first_rows, precision=lax.Precision.HIGHEST
    )
    gram_again = lax.psum(local_second, "row")
    cross_cols = lax.psum_scatter(local_cross, "row", scatter_dimension=2, tiled=True)
    lower_second = jnp.linalg.cholesky(jnp.where(refresh_cube, gram_again, identity))
    fresh_basis = lax.linalg.triangular_solve(
        lower_second, first_rows, left_side=False, lower=True, transpose_a=True
    )
    half_solved = lax.linalg.triangular_solve(lower_first, cross_cols, left_side=True, lower=True)
    fresh_rot = lax.linalg.triangular_solve(lower_second, half_solved, left_side=True, lower=True)
    new_basis = jnp.where(
        refresh_cube, fresh_basis, jnp.where(live_cube, basis.astype(jnp.float32), 0.0)
    )
    rotated = jnp.where(refresh_cube, fresh_rot, jnp.where(live_cube, cross_cols, 0.0)) * norm_scale
    return (new_basis, rotated)


def solution(mesh):
    placed = (P("expert", "row", None), P("expert", "row", None), P("expert"), P("expert"))
    return jax.shard_map(
        on_device,
        mesh=mesh,
        in_specs=placed,
        out_specs=(P("expert", "row", None), P("expert", None, "row")),
        check_vma=False,
    )
```

profile of v0, /device:TPU:0, one launch (start us, length us, event | category | flops | bytes accessed | tf_op | source)
XLA Modules:
  0.0 307.3 jit_solution(6141670956639925859)
XLA Ops:
  7.2 6.8 %fusion.4 = f32[2048,256]{1,0:T(8,128)} fusion(bf16[1,1792,2048]{2,1,0:T(8,128)(2,1)} %param.9, bf16[1,1792,256]{2,1,0:T(8,128)(2,1)} %param.10), kind=kOutput, calls=%fused_computation.9 | convolution fusion | flops 1879048192 | bytes 10354688 | tf_op jit(solution)/shard_map/cds,cdk->csk/dot_general | solution.py:23
  17.7 68.7 %all-reduce.5.cloned.1.call-done = f32[2048,256]{1,0:T(8,128)} async-done(((f32[2048,256]{1,0:T(8,128)}), f32[2048,256]{1,0:T(8,128)}) %all-reduce.5.cloned.1.call-update) | async-done | bytes 2097168 | tf_op jit(solution)/shard_map/psum | solution.py:24
  86.4 5.7 %convolution_select_fusion = f32[256,256]{0,1:T(8,128)S(1)} fusion(f32[2048,256]{1,0:T(8,128)} %all-reduce.5.cloned.1.call-done, pred[]{:T(512)} %bitcast), kind=kOutput, calls=%fused_computation.32 | convolution fusion | flops 1610809344 | bytes 2359297 | tf_op jit(solution)/shard_map/csk,csj->ckj/dot_general | solution.py:25
  93.0 11.7 %custom-call.21 = f32[1,128,128]{2,1,0:T(8,128)S(1)} custom-call(f32[1,128,128]{2,1,0:T(8,128)S(1)} %cholesky.191), custom_call_target="Cholesky" | custom-call | tf_op jit(solution)/shard_map/jit(cholesky)/cholesky | solution.py:33
  104.7 9.8 %custom-call.22 = f32[1,1,128,128]{2,3,1,0:T(8,128)S(1)} custom-call(f32[1,1,128,128]{3,2,1,0:T(8,128)S(1)} %get-tuple-element.68), custom_call_target="InvertDiagBlocksLowerTriangular" | custom-call | tf_op jit(solution)/shard_map/jit(cholesky)/cholesky | solution.py:33
  116.7 11.9 %custom-call.23 = f32[1,128,128]{2,1,0:T(8,128)S(1)} custom-call(f32[1,128,128]{2,1,0:T(8,128)S(1)} %fusion.27), custom_call_target="Cholesky" | custom-call | tf_op jit(solution)/shard_map/jit(cholesky)/cholesky | solution.py:33
  130.7 3.9 %while.8 = (s32[]{:T(128)}, f32[1,256,256]{2,1,0:T(8,128)S(1)}, s32[2,2]{1,0:T(2,128)S(1)}, f32[2,1,128,128]{3,2,1,0:T(8,128)S(1)}, s32[]{:T(128)}) while((s32[]{:T(128)}, f32[1,256,256]{2,1,0:T(8,128)S(1)}, s32[2,2]{1,0:T(2,128)S(1)}, f32[2,1,128,128]{3,2,1,0:T(8,128)S(1)}, s32[]{:T(128)}) %tuple.57), condition=%wide.while_cond, body=%wide.while_body.sunk | while | flops 2 | bytes 131181 | solution.py:34
  131.3 1.4 bitcast_dynamic-update-slice_fusion.6
  134.6 19.7 %custom-call.24 = f32[1,2,128,128]{2,3,1,0:T(8,128)S(1)} custom-call(f32[1,2,128,128]{3,2,1,0:T(8,128)S(1)} %bitcast.221), custom_call_target="InvertDiagBlocksLowerTriangular" | custom-call | tf_op jit(solution)/shard_map/triangular_solve/custom-call.0 | solution.py:34
  154.3 6.2 %fusion.53 = (f32[1,1792,256]{1,2,0:T(8,128)S(1)}, bf16[1,1792,256]{1,2,0:T(8,128)(2,1)}) fusion(bf16[1,1792,2048]{2,1,0:T(8,128)(2,1)} %param.9, f32[2048,256]{1,0:T(8,128)S(1)} %copy-done), kind=kOutput, calls=%fused_computation.99 | convolution fusion | flops 1880489984 | bytes 12189696 | tf_op jit(solution)/shard_map/cds,csk->cdk/dot_general | solution.py:27
  163.4 2.4 fusion.22
  165.9 6.8 %fusion.6 = f32[1,256,2048]{2,1,0:T(8,128)} fusion(bf16[1,1792,2048]{2,1,0:T(8,128)(2,1)} %param.9, bf16[1,1792,256]{1,2,0:T(8,128)(2,1)} %get-tuple-element.70, bf16[1,1792,256]{1,2,0:T(8,128)(2,1)S(1)} %copy.12, pred[]{:T(512)} %bitcast), kind=kOutput, calls=%fused_computation.11 | convolution fusion | flops 1879506944 | bytes 11272193 | tf_op jit(solution)/shard_map/cdk,cds->cks/dot_general | solution.py:31
  172.7 7.5 %select_reduce_fusion = f32[]{:T(128)} fusion(bf16[1,1792,2048]{2,1,0:T(8,128)(2,1)} %param.9, pred[]{:T(512)} %bitcast.40), kind=kLoop, calls=%fused_computation.4 | loop fusion | flops 14680063 | bytes 7340037 | tf_op jit(solution)/shard_map/reduce_sum | solution.py:17
  180.2 39.4 %all-reduce.1 = (f32[]{:T(128)}, f32[]{:T(128)}) all-reduce(f32[]{:T(128)} %select_reduce_fusion, f32[]{:T(128)S(6)} %mul.13), channel_id=1, replica_groups=mesh['expert'=8,'row'=4] {'expert','row'}, use_global_device_ids=true, to_apply=%region_8.12 | all-reduce | flops 2 | bytes 16 | tf_op jit(solution)/shard_map/psum | solution.py:19
  223.1 12.3 %custom-call.25 = f32[1,128,128]{2,1,0:T(8,128)} custom-call(f32[1,128,128]{2,1,0:T(8,128)S(1)} %cholesky.194), custom_call_target="Cholesky" | custom-call | tf_op jit(solution)/shard_map/jit(cholesky)/cholesky | solution.py:42
  236.3 1.5 select_reduce_fusion.2
  237.8 11.3 %custom-call.26 = f32[1,1,128,128]{2,3,1,0:T(8,128)} custom-call(f32[1,1,128,128]{3,2,1,0:T(8,128)} %get-tuple-element.64), custom_call_target="InvertDiagBlocksLowerTriangular" | custom-call | tf_op jit(solution)/shard_map/jit(cholesky)/cholesky | solution.py:42
  251.1 12.5 %custom-call.27 = f32[1,128,128]{2,1,0:T(8,128)S(1)} custom-call(f32[1,128,128]{2,1,0:T(8,128)} %fusion.28), custom_call_target="Cholesky" | custom-call | tf_op jit(solution)/shard_map/jit(cholesky)/cholesky | solution.py:42
  266.3 4.0 %while.9 = (s32[]{:T(128)}, f32[1,256,256]{2,1,0:T(8,128)S(1)}, s32[2,2]{1,0:T(2,128)S(1)}, f32[2,1,128,128]{3,2,1,0:T(8,128)S(1)}, s32[]{:T(128)}) while((s32[]{:T(128)}, f32[1,256,256]{2,1,0:T(8,128)S(1)}, s32[2,2]{1,0:T(2,128)S(1)}, f32[2,1,128,128]{3,2,1,0:T(8,128)S(1)}, s32[]{:T(128)}) %tuple.69), condition=%wide.while_cond.clone, body=%wide.while_body.clone.sunk | while | flops 2 | bytes 131181 | solution.py:43
  266.9 1.4 bitcast_dynamic-update-slice_fusion.7
  268.9 1.4 bitcast_dynamic-update-slice_fusion.7
  270.3 19.9 %custom-call.28 = f32[1,2,128,128]{2,3,1,0:T(8,128)S(1)} custom-call(f32[1,2,128,128]{3,2,1,0:T(8,128)S(1)} %bitcast.220), custom_call_target="InvertDiagBlocksLowerTriangular" | custom-call | tf_op jit(solution)/shard_map/triangular_solve/custom-call.0 | solution.py:43
  293.3 1.7 copy.14
  295.0 1.4 fusion.38
  (68 shorter events, 26.1 us)
Async XLA Ops:
  7.2 79.2 %all-reduce.5.cloned.1.call-start = ((), (), s32[]{:S(2)}) async-start(), calls=%async_computation.1 | async-start | bytes 4194304 | tf_op jit(solution)/shard_map/psum | solution.py:24
  14.0 1.2 copy-start.2
  14.1 206.9 %all-reduce.7.cloned.1.call-start = ((), (), s32[]{:S(2)}) async-start(), calls=%async_computation.2 | async-start | bytes 524288 | tf_op jit(solution)/shard_map/psum | solution.py:40
  92.1 62.3 %copy-start = (f32[2048,256]{1,0:T(8,128)S(1)}, f32[2048,256]{1,0:T(8,128)}, u32[]{:S(2)}) copy-start(f32[2048,256]{1,0:T(8,128)} %all-reduce.5.cloned.1.call-done) | copy-start | bytes 6291460
  92.3 0.7 copy-start.3
  154.3 8.1 %copy-start.4 = (f32[1,2,128,128]{2,3,1,0:T(8,128)}, f32[1,2,128,128]{2,3,1,0:T(8,128)S(1)}, u32[]{:S(2)}) copy-start(f32[1,2,128,128]{2,3,1,0:T(8,128)S(1)} %custom-call.24) | copy-start | bytes 393220
  165.8 129.2 %reduce-scatter.2.cloned.1.call-start = ((), (), s32[]{:S(2)}) async-start(), calls=%async_computation.3 | async-start | bytes 2621440 | tf_op jit(solution)/shard_map/reduce_scatter | solution.py:41
  293.3 1.7 copy-start.5
  295.0 4.4 %copy-start.1 = (f32[1,256,512]{2,1,0:T(8,128)S(1)}, f32[1,256,512]{2,1,0:T(8,128)}, u32[]{:S(2)}) copy-start(f32[1,256,512]{2,1,0:T(8,128)} %reduce-scatter.2.cloned.1.call-done) | copy-start | bytes 1572868
Sparse Core Ops, SparseCore 0:
  14.2 72.1 all-reduce.4
  165.9 43.0 all-reduce.6
  211.9 35.2 reduce-scatter.1
where the time goes:
time: 311 us; the launch traced here: 307 us
  other arithmetic  123 us (40%)
  waiting for transfers between devices  68.8 us (22%)
  matrix products  42 us (14%)
  blocking collectives  39.4 us (13%)
  between operations  19.7 us (6%)
  local copies, waits for them, and re-layouts  13.7 us (4%)
    psum x1, waiting for transfers between devices, on_device(): inner_sum = jnp.stack([lax.psum(local_inner[0], 'row')])  68.7 us
    psum x1, blocking collectives, on_device(): lax.psum((squares, leader * live_count.astype(jnp.float32)), ('expert', '...  39.4 us
    another operation x7, other arithmetic, on_device(): jnp.linalg.cholesky(jnp.where(refresh_cube, gram_again, identity))  39 us
    another operation x6, other arithmetic, on_device(): jnp.linalg.cholesky(jnp.where(refresh_cube, inner_gram, identity))  34.1 us
    another operation x2, other arithmetic, on_device(): lax.linalg.triangular_solve(lower_second, first_rows, left_side=False, lo...  20 us
    another operation x3, other arithmetic, on_device(): lax.linalg.triangular_solve(lower_first, power_rows.astype(jnp.float32),...  19.7 us
    reduce_sum x1, other arithmetic, on_device(): jnp.sum(jnp.where(live_cube, jnp.square(grads.astype(jnp.float32)), 0.0))  7.48 us
    dot_general x1, matrix products, on_device(): jnp.einsum('cds,cdk->csk', grads, basis, preferred_element_type=jnp.float32)  6.82 us
  transfers between devices with their start and end apart: 3, of which 1 were waited for; matrix products, arithmetic and copies ran while one was open for 29% of the time, Pallas kernels for 0%

commit v1 on v0

--- a/solution.py
+++ b/solution.py
@@ -16,9 +16,8 @@
     refresh_cube = refresh[:, None, None]
     squares = jnp.sum(jnp.where(live_cube, jnp.square(grads.astype(jnp.float32)), 0.0))
     leader = (lax.axis_index("row") == 0).astype(jnp.float32)
-    total_sq, total_live = lax.psum(
-        (squares, leader * live_count.astype(jnp.float32)), ("expert", "row")
-    )
+    notes_serve = lambda patch: lax.psum(lax.psum(patch, axis_name="expert"), axis_name="row")
+    total_sq, total_live = notes_serve((squares, leader * live_count.astype(jnp.float32)))
     norm_scale = lax.rsqrt(total_sq / (total_live * D * S) + 1e-06)
     local_inner = jnp.einsum("cds,cdk->csk", grads, basis, preferred_element_type=jnp.float32)
     inner_sum = jnp.stack([lax.psum(local_inner[0], "row")])

time: 311 us -> 299 us (0.961)
  blocking collectives: 39.4 us -> 26.1 us
    psum x1 -> x2, blocking collectives: 39.4 us -> 26.1 us  [the longest x1 16.6 us: on_device(): lax.psum(patch, axis_name='expert')]
  transfers between devices with their start and end apart: 3 -> 3, of which waited for: 1 -> 2; matrix products, arithmetic and copies ran while one was open for 29% -> 30% of each run, Pallas kernels for 0% -> 0%
where the time goes in v1:
time: 299 us; the launch traced here: 295 us
  other arithmetic  124 us (41%)
  waiting for transfers between devices  70.3 us (24%)
  matrix products  42 us (14%)
  blocking collectives  26.1 us (9%)
  between operations  19.5 us (7%)
  local copies, waits for them, and re-layouts  13.4 us (4%)
    psum x1, waiting for transfers between devices, on_device(): inner_sum = jnp.stack([lax.psum(local_inner[0], 'row')])  69.1 us
    another operation x7, other arithmetic, on_device(): jnp.linalg.cholesky(jnp.where(refresh_cube, gram_again, identity))  39 us
    another operation x6, other arithmetic, on_device(): jnp.linalg.cholesky(jnp.where(refresh_cube, inner_gram, identity))  34.4 us
    another operation x2, other arithmetic, on_device(): lax.linalg.triangular_solve(lower_second, first_rows, left_side=False, lo...  19.9 us
    another operation x3, other arithmetic, on_device(): lax.linalg.triangular_solve(lower_first, power_rows.astype(jnp.float32),...  19.7 us
    psum x1, blocking collectives, on_device(): lax.psum(patch, axis_name='expert')  16.6 us
    psum x1, blocking collectives, on_device(): lax.psum(lax.psum(patch, axis_name='expert'), axis_name='row')  9.58 us
    reduce_sum x1, other arithmetic, on_device(): jnp.sum(jnp.where(live_cube, jnp.square(grads.astype(jnp.float32)), 0.0))  7.49 us
  transfers between devices with their start and end apart: 3, of which 2 were waited for; matrix products, arithmetic and copies ran while one was open for 30% of the time, Pallas kernels for 0%

profile of v1, /device:TPU:0, one launch (start us, length us, event | category | flops | bytes accessed | tf_op | source)
XLA Modules:
  0.0 295.3 jit_solution(3365604387327791091)
XLA Ops:
  7.2 6.8 %fusion.4 = f32[2048,256]{1,0:T(8,128)} fusion(bf16[1,1792,2048]{2,1,0:T(8,128)(2,1)} %param.9, bf16[1,1792,256]{2,1,0:T(8,128)(2,1)} %param.10), kind=kOutput, calls=%fused_computation.9 | convolution fusion | flops 1879048192 | bytes 10354688 | tf_op jit(solution)/shard_map/cds,cdk->csk/dot_general | solution.py:22
  17.3 69.1 %all-reduce.6.cloned.1.call-done = f32[2048,256]{1,0:T(8,128)} async-done(((f32[2048,256]{1,0:T(8,128)}), f32[2048,256]{1,0:T(8,128)}) %all-reduce.6.cloned.1.call-update) | async-done | bytes 2097168 | tf_op jit(solution)/shard_map/psum | solution.py:23
  86.4 5.7 %convolution_select_fusion = f32[256,256]{0,1:T(8,128)S(1)} fusion(f32[2048,256]{1,0:T(8,128)} %all-reduce.6.cloned.1.call-done, pred[]{:T(512)} %bitcast), kind=kOutput, calls=%fused_computation.32 | convolution fusion | flops 1610809344 | bytes 2359297 | tf_op jit(solution)/shard_map/csk,csj->ckj/dot_general | solution.py:24
  93.0 11.7 %custom-call.21 = f32[1,128,128]{2,1,0:T(8,128)S(1)} custom-call(f32[1,128,128]{2,1,0:T(8,128)S(1)} %cholesky.191), custom_call_target="Cholesky" | custom-call | tf_op jit(solution)/shard_map/jit(cholesky)/cholesky | solution.py:32
  104.8 9.8 %custom-call.22 = f32[1,1,128,128]{2,3,1,0:T(8,128)S(1)} custom-call(f32[1,1,128,128]{3,2,1,0:T(8,128)S(1)} %get-tuple-element.70), custom_call_target="InvertDiagBlocksLowerTriangular" | custom-call | tf_op jit(solution)/shard_map/jit(cholesky)/cholesky | solution.py:32
  116.8 12.1 %custom-call.23 = f32[1,128,128]{2,1,0:T(8,128)S(1)} custom-call(f32[1,128,128]{2,1,0:T(8,128)S(1)} %fusion.27), custom_call_target="Cholesky" | custom-call | tf_op jit(solution)/shard_map/jit(cholesky)/cholesky | solution.py:32
  130.9 3.9 %while.8 = (s32[]{:T(128)}, f32[1,256,256]{2,1,0:T(8,128)S(1)}, s32[2,2]{1,0:T(2,128)S(1)}, f32[2,1,128,128]{3,2,1,0:T(8,128)S(1)}, s32[]{:T(128)}) while((s32[]{:T(128)}, f32[1,256,256]{2,1,0:T(8,128)S(1)}, s32[2,2]{1,0:T(2,128)S(1)}, f32[2,1,128,128]{3,2,1,0:T(8,128)S(1)}, s32[]{:T(128)}) %tuple.57), condition=%wide.while_cond, body=%wide.while_body.sunk | while | flops 2 | bytes 131181 | solution.py:33
  134.9 19.7 %custom-call.24 = f32[1,2,128,128]{2,3,1,0:T(8,128)S(1)} custom-call(f32[1,2,128,128]{3,2,1,0:T(8,128)S(1)} %bitcast.221), custom_call_target="InvertDiagBlocksLowerTriangular" | custom-call | tf_op jit(solution)/shard_map/triangular_solve/custom-call.0 | solution.py:33
  154.6 6.2 %fusion.53 = (f32[1,1792,256]{1,2,0:T(8,128)S(1)}, bf16[1,1792,256]{1,2,0:T(8,128)(2,1)}) fusion(bf16[1,1792,2048]{2,1,0:T(8,128)(2,1)} %param.9, f32[2048,256]{1,0:T(8,128)S(1)} %copy-done), kind=kOutput, calls=%fused_computation.99 | convolution fusion | flops 1880489984 | bytes 12189696 | tf_op jit(solution)/shard_map/cds,csk->cdk/dot_general | solution.py:26
  163.7 2.4 fusion.22
  166.3 6.8 %fusion.6 = f32[1,256,2048]{2,1,0:T(8,128)} fusion(bf16[1,1792,2048]{2,1,0:T(8,128)(2,1)} %param.9, bf16[1,1792,256]{1,2,0:T(8,128)(2,1)} %get-tuple-element.72, bf16[1,1792,256]{1,2,0:T(8,128)(2,1)S(1)} %copy.12, pred[]{:T(512)} %bitcast), kind=kOutput, calls=%fused_computation.11 | convolution fusion | flops 1879506944 | bytes 11272193 | tf_op jit(solution)/shard_map/cdk,cds->cks/dot_general | solution.py:30
  173.1 7.5 %select_reduce_fusion = f32[]{:T(128)} fusion(bf16[1,1792,2048]{2,1,0:T(8,128)(2,1)} %param.9, pred[]{:T(512)} %bitcast.40), kind=kLoop, calls=%fused_computation.4 | loop fusion | flops 14680063 | bytes 7340037 | tf_op jit(solution)/shard_map/reduce_sum | solution.py:17
  180.6 16.6 %all-reduce.1 = (f32[]{:T(128)}, f32[]{:T(128)}) all-reduce(f32[]{:T(128)} %select_reduce_fusion, f32[]{:T(128)S(6)} %mul.13), channel_id=1, replica_groups=mesh['expert'=8,'row'=4] {'expert'}, use_global_device_ids=true, to_apply=%region_8.12 | all-reduce | flops 2 | bytes 16 | tf_op jit(solution)/shard_map/psum | solution.py:19
  197.2 9.6 %all-reduce.2 = (f32[]{:T(128)}, f32[]{:T(128)}) all-reduce(f32[]{:T(128)} %get-tuple-element.55, f32[]{:T(128)} %get-tuple-element.56), channel_id=1, replica_groups=mesh['expert'=8,'row'=4] {'row'}, use_global_device_ids=true, to_apply=%region_9.13 | all-reduce | flops 2 | bytes 16 | tf_op jit(solution)/shard_map/psum | solution.py:19
  211.4 12.3 %custom-call.25 = f32[1,128,128]{2,1,0:T(8,128)} custom-call(f32[1,128,128]{2,1,0:T(8,128)S(1)} %cholesky.194), custom_call_target="Cholesky" | custom-call | tf_op jit(solution)/shard_map/jit(cholesky)/cholesky | solution.py:41
  224.6 1.5 select_reduce_fusion.2
  226.1 11.3 %custom-call.26 = f32[1,1,128,128]{2,3,1,0:T(8,128)} custom-call(f32[1,1,128,128]{3,2,1,0:T(8,128)} %get-tuple-element.66), custom_call_target="InvertDiagBlocksLowerTriangular" | custom-call | tf_op jit(solution)/shard_map/jit(cholesky)/cholesky | solution.py:41
  239.3 12.5 %custom-call.27 = f32[1,128,128]{2,1,0:T(8,128)S(1)} custom-call(f32[1,128,128]{2,1,0:T(8,128)} %fusion.28), custom_call_target="Cholesky" | custom-call | tf_op jit(solution)/shard_map/jit(cholesky)/cholesky | solution.py:41
  254.6 4.0 %while.9 = (s32[]{:T(128)}, f32[1,256,256]{2,1,0:T(8,128)S(1)}, s32[2,2]{1,0:T(2,128)S(1)}, f32[2,1,128,128]{3,2,1,0:T(8,128)S(1)}, s32[]{:T(128)}) while((s32[]{:T(128)}, f32[1,256,256]{2,1,0:T(8,128)S(1)}, s32[2,2]{1,0:T(2,128)S(1)}, f32[2,1,128,128]{3,2,1,0:T(8,128)S(1)}, s32[]{:T(128)}) %tuple.69), condition=%wide.while_cond.clone, body=%wide.while_body.clone.sunk | while | flops 2 | bytes 131181 | solution.py:42
  255.2 1.4 bitcast_dynamic-update-slice_fusion.7
  257.2 1.4 bitcast_dynamic-update-slice_fusion.7
  258.6 19.9 %custom-call.28 = f32[1,2,128,128]{2,3,1,0:T(8,128)S(1)} custom-call(f32[1,2,128,128]{3,2,1,0:T(8,128)S(1)} %bitcast.220), custom_call_target="InvertDiagBlocksLowerTriangular" | custom-call | tf_op jit(solution)/shard_map/triangular_solve/custom-call.0 | solution.py:42
  281.6 1.7 copy.14
  283.2 1.4 fusion.38
  (69 shorter events, 28.4 us)
Async XLA Ops:
  7.2 79.3 %all-reduce.6.cloned.1.call-start = ((), (), s32[]{:S(2)}) async-start(), calls=%async_computation.1 | async-start | bytes 4194304 | tf_op jit(solution)/shard_map/psum | solution.py:23
  14.0 1.2 copy-start.2
  14.1 195.2 %all-reduce.8.cloned.1.call-start = ((), (), s32[]{:S(2)}) async-start(), calls=%async_computation.2 | async-start | bytes 524288 | tf_op jit(solution)/shard_map/psum | solution.py:39
  92.1 62.5 %copy-start = (f32[2048,256]{1,0:T(8,128)S(1)}, f32[2048,256]{1,0:T(8,128)}, u32[]{:S(2)}) copy-start(f32[2048,256]{1,0:T(8,128)} %all-reduce.6.cloned.1.call-done) | copy-start | bytes 6291460
  92.3 0.7 copy-start.3
  154.6 8.1 %copy-start.4 = (f32[1,2,128,128]{2,3,1,0:T(8,128)}, f32[1,2,128,128]{2,3,1,0:T(8,128)S(1)}, u32[]{:S(2)}) copy-start(f32[1,2,128,128]{2,3,1,0:T(8,128)S(1)} %custom-call.24) | copy-start | bytes 393220
  166.1 117.2 %reduce-scatter.2.cloned.1.call-start = ((), (), s32[]{:S(2)}) async-start(), calls=%async_computation.3 | async-start | bytes 2621440 | tf_op jit(solution)/shard_map/reduce_scatter | solution.py:40
  281.5 1.7 copy-start.5
  283.2 4.4 %copy-start.1 = (f32[1,256,512]{2,1,0:T(8,128)S(1)}, f32[1,256,512]{2,1,0:T(8,128)}, u32[]{:S(2)}) copy-start(f32[1,256,512]{2,1,0:T(8,128)} %reduce-scatter.2.cloned.1.call-done) | copy-start | bytes 1572868
Sparse Core Ops, SparseCore 0:
  14.2 72.1 all-reduce.5
  166.2 43.0 all-reduce.7
  212.2 35.3 reduce-scatter.1
